TPU v7x, 32 devices: a whole 2x2x4 slice. The times are simulated.
32 devices in a mesh: row: 4 (over x, core), col: 8 (over z, y).
Axes of the slice: x: 2, y: 2, z: 4, core: 2. Of those that a mesh axis runs over, the one named last changes fastest.
Arguments:
- ancestor_inverse: bfloat16 [24576, 24576], P('row', 'col'), may hold values from -0.0390625 to 0.0390625
- panels: bfloat16 [24576, 3, 512], P(('row', 'col')), may hold values from -1.1953125 to 1.1953125
- diag_inverse: float32 [3, 512, 512], replicated, may hold values from -6 to 6
- tile_mask: int32 [3, 192], replicated, may hold values 0 or 1
Outputs:
- off_diagonal: float32 [24576, 3, 512], P(('row', 'col'))
- diagonal: float32 [3, 512, 512], replicated
All inputs are finite; a program needn't handle non-finite values.
Results may differ from a plain program's by a relative error of at most 0.0003.
Values may be sent and summed in bfloat16 or wider, within the bound.
A program may use at most 192 MiB of HBM per device.

v0:
```python
import jax
import jax.numpy as jnp
from jax import lax
from jax.sharding import PartitionSpec as P


def exchange(partial, axis):
    count = lax.axis_size(axis)
    rows, width = partial.shape
    return lax.psum_scatter(partial, axis, scatter_dimension=0, tiled=True)


def body(ancestor_inverse, panels, diag_inverse, tile_mask):
    row_count = lax.axis_size("row")
    col_count = lax.axis_size("col")
    span = lax.axis_index("row") * col_count + lax.axis_index("col")
    kept_rows = panels.shape[0]
    panel_count = panels.shape[1]
    tile = kept_rows * row_count * col_count // tile_mask.shape[1]
    full_mask = jnp.repeat(tile_mask, tile, axis=1).astype(jnp.bfloat16)
    own_mask = lax.dynamic_slice_in_dim(full_mask, span * kept_rows, kept_rows, 1)
    moves = [
        (index, index % row_count * col_count + index // row_count)
        for index in range(row_count * col_count)
    ]
    masked = [panels[:, p, :] * own_mask[p][:, None] for p in range(panel_count)]
    sent = [lax.ppermute(block, ("row", "col"), moves) for block in masked]
    sides = [lax.all_gather(block, "row", axis=0, tiled=True) for block in sent]
    results, parts = ([], [])
    for p in range(panel_count):
        partial = jnp.dot(ancestor_inverse, sides[p], preferred_element_type=jnp.float32)
        summed = -exchange(partial, "col")
        results.append(summed)
        parts.append(
            lax.dot_general(
                masked[p].astype(jnp.float32),
                summed,
                (((0,), (0,)), ((), ())),
                precision=lax.Precision.HIGHEST,
            )
        )
    off_diagonal = jnp.stack(results, axis=1)
    schur = lax.psum(jnp.stack(parts), ("row", "col"))
    return (off_diagonal, diag_inverse - schur)


def solution(mesh):
    return jax.shard_map(
        body,
        mesh=mesh,
        in_specs=(P("row", "col"), P(("row", "col"), None, None), P(), P()),
        out_specs=(P(("row", "col"), None, None), P()),
        check_vma=False,
    )
```

profile of v0, /device:TPU:0, one launch (start us, length us, event | category | flops | bytes accessed | tf_op | source)
XLA Modules:
  0.0 952.1 jit_solution(13903537531053839367)
XLA Ops:
  7.2 0.0 all-gather.8.cloned.1.call-start
  7.2 0.7 convert_element_type.10
  7.9 0.1 broadcast_bitcast_fusion
  8.1 0.1 copy.9
  8.2 0.1 dynamic-slice_reduce_fusion.2
  8.3 2.0 bitcast_multiply_fusion.2
  10.3 0.0 copy-start.4
  10.3 1.6 collective-permute-start.2
  11.9 0.0 collective-permute-done.2
  11.9 0.0 all-gather.8.cloned.1.call-update
  11.9 0.0 all-gather.4.cloned.1.call-start
  12.0 1.6 collective-permute-start
  13.5 0.0 collective-permute-done
  13.5 0.0 all-gather.4.cloned.1.call-update
  13.6 0.0 all-gather.6.cloned.1.call-start
  13.6 1.5 collective-permute-start.1
  15.1 0.0 all-gather.6.cloned.1.call-update
  15.2 0.0 reduce-scatter.8.cloned.1.call-start
  15.2 86.4 %all-gather.8.cloned.1.call-done = bf16[3072,512]{1,0:T(8,128)(2,1)} async-done(((bf16[768,512]{1,0:T(8,128)(2,1)}), bf16[3072,512]{1,0:T(8,128)(2,1)}) %all-gather.8.cloned.1.call-update) | async-done | bytes 3145744 | tf_op jit(solution)/shard_map/all_gather | solution.py:28
  101.6 27.8 %convolution_bitcast_fusion = f32[6144,512]{0,1:T(8,128)} fusion(bf16[3072,512]{1,0:T(8,128)(2,1)} %all-gather.8.cloned.1.call-done, bf16[6144,3072]{1,0:T(8,128)(2,1)} %param.4), kind=kOutput, calls=%fused_computation | convolution fusion | flops 19327352832 | bytes 53477376 | tf_op jit(solution)/shard_map/dot_general | solution.py:31
  129.4 0.0 reduce-scatter.8.cloned.1.call-update
  129.4 0.2 reduce-scatter.4.cloned.1.call-start
  129.7 5.6 all-gather.4.cloned.1.call-done
  135.3 27.7 %convolution_bitcast_fusion.2 = f32[6144,512]{0,1:T(8,128)} fusion(bf16[3072,512]{1,0:T(8,128)(2,1)} %all-gather.4.cloned.1.call-done, bf16[6144,3072]{1,0:T(8,128)(2,1)} %param.4), kind=kOutput, calls=%fused_computation.2 | convolution fusion | flops 19327352832 | bytes 53477376 | tf_op jit(solution)/shard_map/dot_general | solution.py:31
  163.0 0.0 reduce-scatter.4.cloned.1.call-update
  163.1 0.3 reduce-scatter.6.cloned.1.call-start
  163.3 3.3 all-gather.6.cloned.1.call-done
  166.6 27.7 %convolution_bitcast_fusion.1 = f32[6144,512]{0,1:T(8,128)} fusion(bf16[3072,512]{1,0:T(8,128)(2,1)} %all-gather.6.cloned.1.call-done, bf16[6144,3072]{1,0:T(8,128)(2,1)} %param.4), kind=kOutput, calls=%fused_computation.1 | convolution fusion | flops 19327352832 | bytes 53477376 | tf_op jit(solution)/shard_map/dot_general | solution.py:31
  194.3 0.0 reduce-scatter.6.cloned.1.call-update
  194.3 0.3 all-reduce.2.cloned.1.call-start
  194.6 182.9 %reduce-scatter.8.cloned.1.call-done = f32[768,512]{0,1:T(8,128)} async-done(((f32[6144,512]{0,1:T(8,128)}), f32[768,512]{0,1:T(8,128)}) %reduce-scatter.8.cloned.1.call-update) | async-done | bytes 1572880 | tf_op jit(solution)/shard_map/reduce_scatter | solution.py:10
  377.5 3.1 fusion.12
  380.7 206.9 %reduce-scatter.4.cloned.1.call-done = f32[768,512]{0,1:T(8,128)} async-done(((f32[6144,512]{0,1:T(8,128)}), f32[768,512]{0,1:T(8,128)}) %reduce-scatter.4.cloned.1.call-update) | async-done | bytes 1572880 | tf_op jit(solution)/shard_map/reduce_scatter | solution.py:10
  587.6 3.4 fusion.6
  590.9 206.7 %reduce-scatter.6.cloned.1.call-done = f32[768,512]{0,1:T(8,128)} async-done(((f32[6144,512]{0,1:T(8,128)}), f32[768,512]{0,1:T(8,128)}) %reduce-scatter.6.cloned.1.call-update) | async-done | bytes 1572880 | tf_op jit(solution)/shard_map/reduce_scatter | solution.py:10
  797.6 3.1 fusion.9
  800.7 2.0 pad_maximum_fusion.1
  802.7 0.0 all-reduce.2.cloned.1.call-update
  802.7 1.4 copy-done
  804.1 0.1 negate_bitcast_fusion
  804.2 0.4 copy-done.2
  804.6 0.1 negate_bitcast_fusion.1
  804.7 0.9 copy-done.1
  805.7 0.1 negate_bitcast_fusion.2
  805.8 2.4 pad_maximum_fusion
  808.2 6.2 copy.6
  814.4 126.5 %all-reduce.2.cloned.1.call-done = f32[3,512,512]{2,1,0:T(8,128)} async-done(((f32[3,512,512]{2,1,0:T(8,128)}), f32[3,512,512]{2,1,0:T(8,128)}) %all-reduce.2.cloned.1.call-update) | async-done | bytes 3145744 | tf_op jit(solution)/shard_map/psum | solution.py:43
  941.0 4.3 sub.3
  (7 shorter events, 0.0 us)
Async XLA Ops:
  7.2 94.5 %all-gather.8.cloned.1.call-start = ((), (), s32[]{:S(2)}) async-start(), calls=%async_computation.7 | async-start | bytes 3932160 | tf_op jit(solution)/shard_map/all_gather | solution.py:28
  10.3 119.1 %copy-start.4 = (bf16[768,512]{1,0:T(8,128)(2,1)}, bf16[768,512]{1,0:T(8,128)(2,1)S(1)}, u32[]{:S(2)}) copy-start(bf16[768,512]{1,0:T(8,128)(2,1)S(1)} %get-tuple-element.7) | copy-start | bytes 2359300
  10.3 1.6 collective-permute-start.2
  11.9 123.4 %all-gather.4.cloned.1.call-start = ((), (), s32[]{:S(2)}) async-start(), calls=%async_computation.3 | async-start | bytes 3932160 | tf_op jit(solution)/shard_map/all_gather | solution.py:28
  12.0 1.6 collective-permute-start
  13.6 153.1 %all-gather.6.cloned.1.call-start = ((), (), s32[]{:S(2)}) async-start(), calls=%async_computation.5 | async-start | bytes 3932160 | tf_op jit(solution)/shard_map/all_gather | solution.py:28
  13.6 1.5 collective-permute-start.1
  15.2 362.4 %reduce-scatter.8.cloned.1.call-start = ((), (), s32[]{:S(2)}) async-start(), calls=%async_computation.8 | async-start | bytes 14155776 | tf_op jit(solution)/shard_map/reduce_scatter | solution.py:10
  129.4 458.1 %reduce-scatter.4.cloned.1.call-start = ((), (), s32[]{:S(2)}) async-start(), calls=%async_computation.4 | async-start | bytes 14155776 | tf_op jit(solution)/shard_map/reduce_scatter | solution.py:10
  163.1 634.6 %reduce-scatter.6.cloned.1.call-start = ((), (), s32[]{:S(2)}) async-start(), calls=%async_computation.6 | async-start | bytes 14155776 | tf_op jit(solution)/shard_map/reduce_scatter | solution.py:10
  194.3 746.7 %all-reduce.2.cloned.1.call-start = ((), (), s32[]{:S(2)}) async-start(), calls=%async_computation.9 | async-start | bytes 6291456 | tf_op jit(solution)/shard_map/psum | solution.py:43
  802.7 1.4 copy-start
  802.7 1.9 copy-start.2
  804.1 1.5 copy-start.1
  808.2 132.8 %copy-start.3 = (f32[3,512,512]{2,1,0:T(8,128)S(1)}, f32[3,512,512]{2,1,0:T(8,128)}, u32[]{:S(2)}) copy-start(f32[3,512,512]{2,1,0:T(8,128)} %param.6) | copy-start | bytes 9437188
Sparse Core Ops, SparseCore 0:
  12.0 89.5 all-gather.7
  103.2 32.0 all-gather.3
  136.9 29.7 all-gather.5
  170.0 207.4 reduce-scatter.7
  381.0 206.5 reduce-scatter.3
  591.0 206.5 reduce-scatter.5
  803.7 137.2 all-reduce.1
where the time goes:
time: 953 us; the launch traced here: 952 us
  waiting for transfers between devices  818 us (86%)
  matrix products  92.8 us (10%)
  between operations  14.2 us (1%)
  other arithmetic  11.7 us (1%)
    reduce_scatter x3, waiting for transfers between devices, exchange(): return lax.psum_scatter(partial, axis, scatter_dimension=0, tiled=True)  597 us
    psum x1, waiting for transfers between devices, body(): schur = lax.psum(jnp.stack(parts), ('row', 'col'))  127 us
    all_gather x3, waiting for transfers between devices, body(): sides = [lax.all_gather(block, 'row', axis=0, tiled=True) for block in sent]  95.3 us
    dot_general x3, matrix products, body(): jnp.dot(ancestor_inverse, sides[p], preferred_element_type=jnp.float32)  83.2 us
  transfers between devices with their start and end apart: 10, of which 7 were waited for; matrix products, arithmetic and copies ran while one was open for 10% of the time, Pallas kernels for 0%

commit v1 on v0

--- a/solution.py
+++ b/solution.py
@@ -40,7 +40,7 @@
             )
         )
     off_diagonal = jnp.stack(results, axis=1)
-    schur = lax.psum(jnp.stack(parts), ("row", "col"))
+    schur = jnp.sum(lax.all_gather(jnp.stack(parts), ("row", "col")), axis=0)
     return (off_diagonal, diag_inverse - schur)
 
 

time: 953 us -> 1360 us (1.43)
  waiting for transfers between devices: 818 us -> 1200 us
  other arithmetic: 11.7 us -> 42.5 us
    all_gather x0 -> x1, waiting for transfers between devices: none -> 504 us  [body(): schur = jnp.sum(lax.all_gather(jnp.stack(parts), ('row', 'col')), axis=0)]
    psum x1 -> x0, waiting for transfers between devices: 127 us -> none  [body(): schur = lax.psum(jnp.stack(parts), ('row', 'col'))]
    reduce_sum x0 -> x1, other arithmetic: none -> 30.8 us  [body(): schur = jnp.sum(lax.all_gather(jnp.stack(parts), ('row', 'col')), axis=0)]
  transfers between devices with their start and end apart: 10 -> 10, of which waited for: 7 -> 7; matrix products, arithmetic and copies ran while one was open for 10% -> 7% of each run, Pallas kernels for 0% -> 0%
where the time goes in v1:
time: 1360 us
  waiting for transfers between devices  1200 us (88%)
  matrix products  92.5 us (7%)
  other arithmetic  42.5 us (3%)
  between operations  14.2 us (1%)
    reduce_scatter x3, waiting for transfers between devices, exchange(): return lax.psum_scatter(partial, axis, scatter_dimension=0, tiled=True)  597 us
    all_gather x1, waiting for transfers between devices, body(): schur = jnp.sum(lax.all_gather(jnp.stack(parts), ('row', 'col')), axis=0)  504 us
    all_gather x3, waiting for transfers between devices, body(): sides = [lax.all_gather(block, 'row', axis=0, tiled=True) for block in sent]  95.6 us
    dot_general x3, matrix products, body(): jnp.dot(ancestor_inverse, sides[p], preferred_element_type=jnp.float32)  82.9 us
    reduce_sum x1, other arithmetic, body(): schur = jnp.sum(lax.all_gather(jnp.stack(parts), ('row', 'col')), axis=0)  30.8 us
  transfers between devices with their start and end apart: 10, of which 7 were waited for; matrix products, arithmetic and copies ran while one was open for 7% of the time, Pallas kernels for 0%

profile of v1, /device:TPU:0, one launch (start us, length us, event | category | flops | bytes accessed | tf_op | source)
XLA Modules:
  0.0 1360.4 jit_solution(12932539839666719789)
XLA Ops:
  7.2 0.0 all-gather.8.cloned.1.call-start
  7.2 0.7 convert_element_type.10
  7.9 0.1 broadcast_bitcast_fusion
  8.1 0.1 copy.10
  8.2 0.1 dynamic-slice_reduce_fusion.2
  8.3 2.0 bitcast_multiply_fusion.2
  10.3 0.0 copy-start.3
  10.3 1.6 collective-permute-start.1
  11.9 0.0 all-gather.8.cloned.1.call-update
  11.9 0.0 all-gather.10.cloned.1.call-start
  12.0 1.5 collective-permute-start.2
  13.5 0.0 collective-permute-done.2
  13.5 0.0 all-gather.10.cloned.1.call-update
  13.5 0.0 all-gather.6.cloned.1.call-start
  13.6 1.5 collective-permute-start
  15.1 0.0 all-gather.6.cloned.1.call-update
  15.1 0.0 reduce-scatter.6.cloned.1.call-start
  15.2 86.4 %all-gather.8.cloned.1.call-done = bf16[3072,512]{1,0:T(8,128)(2,1)} async-done(((bf16[768,512]{1,0:T(8,128)(2,1)}), bf16[3072,512]{1,0:T(8,128)(2,1)}) %all-gather.8.cloned.1.call-update) | async-done | bytes 3145744 | tf_op jit(solution)/shard_map/all_gather | solution.py:28
  101.6 27.7 %convolution_bitcast_fusion.1 = f32[6144,512]{0,1:T(8,128)} fusion(bf16[3072,512]{1,0:T(8,128)(2,1)} %all-gather.8.cloned.1.call-done, bf16[6144,3072]{1,0:T(8,128)(2,1)} %param.4), kind=kOutput, calls=%fused_computation.1 | convolution fusion | flops 19327352832 | bytes 53477376 | tf_op jit(solution)/shard_map/dot_general | solution.py:31
  129.3 0.0 reduce-scatter.6.cloned.1.call-update
  129.4 0.2 reduce-scatter.8.cloned.1.call-start
  129.6 5.7 all-gather.10.cloned.1.call-done
  135.3 27.6 %convolution_bitcast_fusion = f32[6144,512]{0,1:T(8,128)} fusion(bf16[3072,512]{1,0:T(8,128)(2,1)} %all-gather.10.cloned.1.call-done, bf16[6144,3072]{1,0:T(8,128)(2,1)} %param.4), kind=kOutput, calls=%fused_computation | convolution fusion | flops 19327352832 | bytes 53477376 | tf_op jit(solution)/shard_map/dot_general | solution.py:31
  162.9 0.0 reduce-scatter.8.cloned.1.call-update
  162.9 0.3 reduce-scatter.4.cloned.1.call-start
  163.2 3.4 all-gather.6.cloned.1.call-done
  166.6 27.6 %convolution_bitcast_fusion.2 = f32[6144,512]{0,1:T(8,128)} fusion(bf16[3072,512]{1,0:T(8,128)(2,1)} %all-gather.6.cloned.1.call-done, bf16[6144,3072]{1,0:T(8,128)(2,1)} %param.4), kind=kOutput, calls=%fused_computation.2 | convolution fusion | flops 19327352832 | bytes 53477376 | tf_op jit(solution)/shard_map/dot_general | solution.py:31
  194.2 0.0 reduce-scatter.4.cloned.1.call-update
  194.3 0.3 all-gather.12.cloned.1.call-start
  194.6 183.0 %reduce-scatter.6.cloned.1.call-done = f32[768,512]{0,1:T(8,128)} async-done(((f32[6144,512]{0,1:T(8,128)}), f32[768,512]{0,1:T(8,128)}) %reduce-scatter.6.cloned.1.call-update) | async-done | bytes 1572880 | tf_op jit(solution)/shard_map/reduce_scatter | solution.py:10
  377.5 3.1 fusion.9
  380.7 206.9 %reduce-scatter.8.cloned.1.call-done = f32[768,512]{0,1:T(8,128)} async-done(((f32[6144,512]{0,1:T(8,128)}), f32[768,512]{0,1:T(8,128)}) %reduce-scatter.8.cloned.1.call-update) | async-done | bytes 1572880 | tf_op jit(solution)/shard_map/reduce_scatter | solution.py:10
  587.6 3.4 fusion.12
  590.9 206.7 %reduce-scatter.4.cloned.1.call-done = f32[768,512]{0,1:T(8,128)} async-done(((f32[6144,512]{0,1:T(8,128)}), f32[768,512]{0,1:T(8,128)}) %reduce-scatter.4.cloned.1.call-update) | async-done | bytes 1572880 | tf_op jit(solution)/shard_map/reduce_scatter | solution.py:10
  797.6 3.1 fusion.6
  800.7 2.0 pad_maximum_fusion.1
  802.7 0.0 all-gather.12.cloned.1.call-update
  802.7 1.4 copy-done
  804.1 0.1 negate_bitcast_fusion.1
  804.2 0.4 copy-done.1
  804.6 0.1 negate_bitcast_fusion
  804.7 0.9 copy-done.2
  805.6 0.1 negate_bitcast_fusion.2
  805.8 2.4 pad_maximum_fusion
  808.2 6.5 copy.7
  814.7 503.8 %all-gather.12.cloned.1.call-done = f32[96,512,512]{2,1,0:T(8,128)} async-done(((f32[3,512,512]{2,1,0:T(8,128)}), f32[96,512,512]{2,1,0:T(8,128)}) %all-gather.12.cloned.1.call-update) | async-done | bytes 100663312 | tf_op jit(solution)/shard_map/all_gather | solution.py:43
  1318.5 30.8 %reduce_sum.9 = f32[3,512,512]{2,1,0:T(8,128)S(1)} reduce(f32[32,3,512,512]{3,2,1,0:T(8,128)} %bitcast.12, f32[]{:T(128)} %constant.17.clone.1), dimensions={0}, to_apply=%region_3.0 | reduce | flops 24379392 | bytes 103809024 | tf_op jit(solution)/shard_map/reduce_sum | solution.py:43
  1349.3 4.3 sub.3
  (6 shorter events, 0.0 us)
Async XLA Ops:
  7.2 94.5 %all-gather.8.cloned.1.call-start = ((), (), s32[]{:S(2)}) async-start(), calls=%async_computation.5 | async-start | bytes 3932160 | tf_op jit(solution)/shard_map/all_gather | solution.py:28
  10.3 119.0 %copy-start.3 = (bf16[768,512]{1,0:T(8,128)(2,1)}, bf16[768,512]{1,0:T(8,128)(2,1)S(1)}, u32[]{:S(2)}) copy-start(bf16[768,512]{1,0:T(8,128)(2,1)S(1)} %get-tuple-element.10) | copy-start | bytes 2359300
  10.3 1.6 collective-permute-start.1
  11.9 123.4 %all-gather.10.cloned.1.call-start = ((), (), s32[]{:S(2)}) async-start(), calls=%async_computation.7 | async-start | bytes 3932160 | tf_op jit(solution)/shard_map/all_gather | solution.py:28
  12.0 1.5 collective-permute-start.2
  13.5 153.1 %all-gather.6.cloned.1.call-start = ((), (), s32[]{:S(2)}) async-start(), calls=%async_computation.3 | async-start | bytes 3932160 | tf_op jit(solution)/shard_map/all_gather | solution.py:28
  13.6 1.5 collective-permute-start
  15.1 362.4 %reduce-scatter.6.cloned.1.call-start = ((), (), s32[]{:S(2)}) async-start(), calls=%async_computation.6 | async-start | bytes 14155776 | tf_op jit(solution)/shard_map/reduce_scatter | solution.py:10
  129.4 458.2 %reduce-scatter.8.cloned.1.call-start = ((), (), s32[]{:S(2)}) async-start(), calls=%async_computation.8 | async-start | bytes 14155776 | tf_op jit(solution)/shard_map/reduce_scatter | solution.py:10
  162.9 634.7 %reduce-scatter.4.cloned.1.call-start = ((), (), s32[]{:S(2)}) async-start(), calls=%async_computation.4 | async-start | bytes 14155776 | tf_op jit(solution)/shard_map/reduce_scatter | solution.py:10
  194.3 1124.2 %all-gather.12.cloned.1.call-start = ((), (), s32[]{:S(2)}) async-start(), calls=%async_computation.9 | async-start | bytes 103809024 | tf_op jit(solution)/shard_map/all_gather | solution.py:43
  802.7 1.4 copy-start
  802.7 1.9 copy-start.1
  804.1 1.5 copy-start.2
Sparse Core Ops, SparseCore 0:
  12.0 89.5 all-gather.7
  103.2 32.0 all-gather.9
  136.9 29.7 all-gather.5
  170.0 207.4 reduce-scatter.5
  381.0 206.5 reduce-scatter.7
  591.0 206.5 reduce-scatter.3
  802.9 515.5 all-gather.11
